TPU v7x, 32 devices: a whole 2x2x4 slice. The times are simulated.
32 devices in a mesh: node: 16 (over z, x, core), col: 2 (over y).
Axes of the slice: x: 2, y: 2, z: 4, core: 2. Of those that a mesh axis runs over, the one named last changes fastest.
Arguments:
- coefficients: float32 [2, 64, 256, 1024], P('col', 'node'), may hold values from -6 to 6
- self_weights: bfloat16 [2, 6, 64, 256, 256], P('col', None, 'node'), may hold values from -0.25 to 0.25
- cross_weights: bfloat16 [2, 6, 64, 256, 256], P('col', None, 'node'), may hold values from -0.25 to 0.25
- true_ranks: int32 [2, 64], P('col', 'node'), may hold values from 128 to 256
Outputs:
- field: float32 [64, 256, 1024], P('node', None, 'col')
Inputs may be any that keep to these rules, and one draw needn't show every extreme that they name: `true_ranks`: each node's true rank within its padded rank 256.
All inputs are finite; a program needn't handle non-finite values.
Results may differ from a plain program's by a relative error of at most 0.0003.
Values sent between devices are 32-bit elements; how exact they have to be, the bound alone decides.
A program may use at most 64 MiB of HBM per device.

v0:
```python
import functools

import jax
import jax.numpy as jnp
from jax import lax
from jax.experimental import pallas as pl
from jax.experimental.pallas import tpu as pltpu
from jax.sharding import PartitionSpec as P

WIDTH = 128
LAG = 4


def flip(index, mask):
    return index + mask * (1 - 2 * ((index // mask) % 2))


def split(state):
    high = state.astype(jnp.bfloat16)
    low = (state - high.astype(jnp.float32)).astype(jnp.bfloat16)
    return high, low


def product(weights, parts):
    high, low = parts
    return jnp.dot(weights, high, preferred_element_type=jnp.float32) + jnp.dot(
        weights, low, preferred_element_type=jnp.float32
    )


def kernel(
    cols, nodes, levels, width, shard,
    coeff, self_hbm, cross_hbm, ranks, out,
    acc, tmp, self_w, cross_w, send, recv, col_send, col_recv, end_send, end_recv,
    own_rank, other_rank,
    load_sem, weight_sem, send_sem, recv_sem, col_send_sem, col_recv_sem,
    end_send_sem, end_recv_sem, rank_sem,
):
    rank_rows = acc.shape[1]
    local_bits = nodes.bit_length() - 1
    hops = levels - local_bits
    pieces = shard // width
    chunks = cols * pieces
    items = chunks * nodes
    theirs = (cols - 1) * pieces * nodes
    me = lax.axis_index("node")
    my_col = lax.axis_index("col")
    peers = [flip(me, 1 << hop) for hop in range(hops)]

    def load(chunk):
        column = (my_col + 1 + chunk % cols) % cols
        start = pl.multiple_of(column * shard + (chunk // cols) * width, width)
        return pltpu.make_async_copy(
            coeff.at[0, :, :, pl.ds(start, width)],
            acc.at[pl.ds(chunk * nodes, nodes)],
            load_sem.at[chunk],
        )

    def weight_loads(level):
        return (
            pltpu.make_async_copy(self_hbm.at[0, level], self_w.at[level], weight_sem.at[0, level]),
            pltpu.make_async_copy(cross_hbm.at[0, level], cross_w.at[level], weight_sem.at[1, level]),
        )

    def hop_copy(hop, item):
        return pltpu.make_async_remote_copy(
            src_ref=send.at[hop, item],
            dst_ref=recv.at[hop, item],
            send_sem=send_sem.at[hop, item],
            recv_sem=recv_sem.at[hop, item],
            device_id={"node": peers[hop]},
            device_id_type=pl.DeviceIdType.MESH,
        )

    def col_copy(item):
        column = (my_col + 1 + (item // nodes) % (cols - 1)) % cols
        return pltpu.make_async_remote_copy(
            src_ref=col_send.at[item],
            dst_ref=col_recv.at[item],
            send_sem=col_send_sem.at[item],
            recv_sem=col_recv_sem.at[item],
            device_id={"col": column},
            device_id_type=pl.DeviceIdType.MESH,
        )

    def end_copy(place):
        return pltpu.make_async_remote_copy(
            src_ref=end_send.at[place],
            dst_ref=end_recv.at[place],
            send_sem=end_send_sem.at[place],
            recv_sem=end_recv_sem.at[place],
            device_id={"node": peers[hops - 1]},
            device_id_type=pl.DeviceIdType.MESH,
        )

    rank_copy = pltpu.make_async_remote_copy(
        src_ref=own_rank,
        dst_ref=other_rank,
        send_sem=rank_sem.at[0],
        recv_sem=rank_sem.at[1],
        device_id={"node": peers[hops - 1]},
        device_id_type=pl.DeviceIdType.MESH,
    )

    load(0).start()
    for level in range(local_bits + 1):
        for copy in weight_loads(level):
            copy.start()
    for chunk in range(1, chunks):
        load(chunk).start()
    for level in range(local_bits + 1, levels):
        for copy in weight_loads(level):
            copy.start()

    barrier = pltpu.get_barrier_semaphore()
    for peer in peers:
        pl.semaphore_signal(barrier, inc=1, device_id={"node": peer}, device_id_type=pl.DeviceIdType.MESH)
    for step in range(1, cols):
        pl.semaphore_signal(
            barrier, inc=1, device_id={"col": (my_col + step) % cols}, device_id_type=pl.DeviceIdType.MESH
        )
    for node in range(nodes):
        own_rank[node] = jnp.full(own_rank.shape[1:], ranks[0, node], jnp.int32)
    pl.semaphore_wait(barrier, hops + cols - 1)
    rank_copy.start()

    row = lax.broadcasted_iota(jnp.int32, (rank_rows, width), 0)

    def masked(values, rank_tile):
        return jnp.where(row < rank_tile[0:1, :], values, 0.0)

    def first(chunk):
        base = chunk * nodes
        load(chunk).wait()

        def at(bank, node):
            return acc.at[base + node] if bank == 0 else tmp.at[node]

        for level in range(local_bits):

            @pl.when(chunk == 0)
            def _():
                for copy in weight_loads(level):
                    copy.wait()

            def body(node, _):
                other = flip(node, 1 << level)
                value = product(self_w[level, node], split(at(level % 2, node)[...]))
                value += product(cross_w[level, other], split(at(level % 2, other)[...]))
                at((level + 1) % 2, node)[...] = masked(value, own_rank[node])
                return 0

            lax.fori_loop(0, nodes, body, 0)

        @pl.when(chunk == 0)
        def _():
            for copy in weight_loads(local_bits):
                copy.wait()

        def body(node, _):
            parts = split(at(local_bits % 2, node)[...])
            send[0, base + node] = product(cross_w[local_bits, node], parts)
            hop_copy(0, base + node).start()
            acc[base + node] = product(self_w[local_bits, node], parts)
            return 0

        lax.fori_loop(0, nodes, body, 0)

    def combine(hop, item):
        level = local_bits + hop

        @pl.when(item == 0)
        def _():
            for copy in weight_loads(level):
                copy.wait()

        hop_copy(hop - 1, item).wait_recv()
        node = item % nodes
        return node, level, split(masked(acc[item] + recv[hop - 1, item], own_rank[node]))

    def middle(hop, item):
        node, level, parts = combine(hop, item)
        send[hop, item] = product(cross_w[level, node], parts)
        hop_copy(hop, item).start()
        acc[item] = product(self_w[level, node], parts)

    def last(item):
        node, level, parts = combine(hops - 1, item)

        @pl.when(item == 0)
        def _():
            rank_copy.wait()

        sent = masked(product(cross_w[level, node], parts), other_rank[node])
        kept = masked(product(self_w[level, node], parts), own_rank[node])

        chunk = item // nodes
        piece = chunk // cols

        @pl.when(chunk % cols < cols - 1)
        def _():
            slot = (piece * (cols - 1) + chunk % cols) * nodes + node
            col_send[slot, 0] = kept
            col_send[slot, 1] = sent
            col_copy(slot).start()

        @pl.when(chunk % cols == cols - 1)
        def _():
            place = piece * nodes + node
            total_kept, total_sent = kept, sent
            for step in range(cols - 1):
                slot = (piece * (cols - 1) + step) * nodes + node
                col_copy(slot).wait_recv()
                total_kept += col_recv[slot, 0]
                total_sent += col_recv[slot, 1]
            end_send[place] = total_sent
            end_copy(place).start()
            acc[item] = total_kept

    def finish(item):
        node = item % nodes
        piece = item // (nodes * cols)
        place = piece * nodes + node
        end_copy(place).wait_recv()
        start = pl.multiple_of(piece * width, width)
        out[node, :, pl.ds(start, width)] = acc[item] + end_recv[place]

    def tick(time, _):
        @pl.when((time < items) & (time % nodes == 0))
        def _():
            first(time // nodes)

        for hop in range(1, hops):
            item = time - (1 + (hop - 1) * LAG)

            @pl.when((item >= 0) & (item < items))
            def _():
                if hop == hops - 1:
                    last(item)
                else:
                    middle(hop, item)

        done = time - (1 + (hops - 1) * LAG)

        @pl.when((done >= 0) & ((done // nodes) % cols == cols - 1))
        def _():
            finish(done)

        return 0

    lax.fori_loop(0, items + 1 + (hops - 1) * LAG, tick, 0)

    def drain_hops(item, _):
        for hop in range(hops - 1):
            hop_copy(hop, item).wait_send()
        return 0

    def drain_cols(item, _):
        col_copy(item).wait_send()
        return 0

    def drain_end(place, _):
        end_copy(place).wait_send()
        return 0

    lax.fori_loop(0, items, drain_hops, 0)
    lax.fori_loop(0, theirs, drain_cols, 0)
    lax.fori_loop(0, items - theirs, drain_end, 0)


def shards(cols, coefficients, self_weights, cross_weights, true_ranks):
    nodes, rank, illum = coefficients.shape[1:]
    levels = self_weights.shape[1]
    shard = illum // cols
    width = min(WIDTH, shard)
    items = illum // width * nodes
    mine = shard // width * nodes
    theirs = items - mine
    hops = levels - (nodes.bit_length() - 1)
    tile = (rank, width)
    dma = pltpu.SemaphoreType.DMA
    return pl.pallas_call(
        functools.partial(kernel, cols, nodes, levels, width, shard),
        out_shape=jax.ShapeDtypeStruct((nodes, rank, shard), jnp.float32),
        in_specs=[pl.BlockSpec(memory_space=pl.ANY)] * 3 + [pl.BlockSpec(memory_space=pltpu.SMEM)],
        out_specs=pl.BlockSpec(memory_space=pltpu.VMEM),
        scratch_shapes=[
            pltpu.VMEM((items, *tile), jnp.float32),
            pltpu.VMEM((nodes, *tile), jnp.float32),
            pltpu.VMEM((levels, nodes, rank, rank), jnp.bfloat16),
            pltpu.VMEM((levels, nodes, rank, rank), jnp.bfloat16),
            pltpu.VMEM((hops - 1, items, *tile), jnp.float32),
            pltpu.VMEM((hops - 1, items, *tile), jnp.float32),
            pltpu.VMEM((theirs, 2, *tile), jnp.float32),
            pltpu.VMEM((theirs, 2, *tile), jnp.float32),
            pltpu.VMEM((mine, *tile), jnp.float32),
            pltpu.VMEM((mine, *tile), jnp.float32),
            pltpu.VMEM((nodes, 8, width), jnp.int32),
            pltpu.VMEM((nodes, 8, width), jnp.int32),
            dma((items // nodes,)),
            dma((2, levels)),
            dma((hops - 1, items)),
            dma((hops - 1, items)),
            dma((theirs,)),
            dma((theirs,)),
            dma((mine,)),
            dma((mine,)),
            dma((2,)),
        ],
        compiler_params=pltpu.CompilerParams(
            collective_id=0, has_side_effects=True, vmem_limit_bytes=60 * 1024 * 1024
        ),
    )(coefficients, self_weights, cross_weights, true_ranks)


def solution(mesh):
    placed = (
        P("col", "node", None, None),
        P("col", None, "node", None, None),
        P("col", None, "node", None, None),
        P("col", "node"),
    )
    return jax.shard_map(
        functools.partial(shards, mesh.shape["col"]),
        mesh=mesh, in_specs=placed, out_specs=P("node", None, "col"), check_vma=False,
    )
```

profile of v0, /device:TPU:0, one launch (start us, length us, event | category | flops | bytes accessed | tf_op | source)
XLA Modules:
  0.0 166.7 jit_solution(10129780980234509779)
XLA Ops:
  0.0 163.6 %shard_map.46 = f32[4,256,512]{2,1,0:T(8,128)} custom-call(f32[1,4,256,1024]{3,2,1,0:T(8,128)} %coeff.1, bf16[1,6,4,256,256]{4,3,2,1,0:T(8,128)(2,1)} %self_hbm.1, bf16[1,6,4,256,256]{4,3,2,1,0:T(8,128)(2,1)} %cross_hbm.1, s32[1,4]{1,0:T(1,128)} %ranks.1), custom_call_target="tpu_custom_call" | custom-call | tf_op jit(solution)/shard_map/pallas_call | solution.py:282
  163.6 3.1 %copy.6 = f32[4,256,512]{2,1,0:T(8,128)} copy(f32[4,256,512]{2,1,0:T(8,128)} %shard_map.46) | data formatting | bytes 4194304
where the time goes:
time: 167 us
  Pallas kernels  164 us (98%)
  local copies, waits for them, and re-layouts  3.08 us (2%)
    pallas_call x1, Pallas kernels, shards(): pl.pallas_call(functools.partial(kernel, cols, nodes, levels, width, shar...  164 us

commit v1 on v0

--- a/solution.py
+++ b/solution.py
@@ -308,7 +308,7 @@
             dma((2,)),
         ],
         compiler_params=pltpu.CompilerParams(
-            collective_id=0, has_side_effects=True, vmem_limit_bytes=60 * 1024 * 1024
+            collective_id=0, has_side_effects=True, vmem_limit_bytes=51 * 1024 * 1024
         ),
     )(coefficients, self_weights, cross_weights, true_ranks)
 

time: 167 us -> 164 us (0.982)
  Pallas kernels: 164 us -> 162 us
where the time goes in v1:
time: 164 us
  Pallas kernels  162 us (99%)
  local copies, waits for them, and re-layouts  1.98 us (1%)
    pallas_call x1, Pallas kernels, shards(): pl.pallas_call(functools.partial(kernel, cols, nodes, levels, width, shar...  162 us

profile of v1, /device:TPU:0, one launch (start us, length us, event | category | flops | bytes accessed | tf_op | source)
XLA Modules:
  0.0 164.1 jit_solution(6923754756827013097)
XLA Ops:
  0.0 0.0 copy-start
  0.0 0.7 copy-done
  0.7 162.1 %shard_map.46 = f32[4,256,512]{2,1,0:T(8,128)S(1)} custom-call(f32[1,4,256,1024]{3,2,1,0:T(8,128)} %coeff.1, bf16[1,6,4,256,256]{4,3,2,1,0:T(8,128)(2,1)} %self_hbm.1, bf16[1,6,4,256,256]{4,3,2,1,0:T(8,128)(2,1)} %cross_hbm.1, s32[1,4]{1,0:T(1,128)S(1)} %copy-done), custom_call_target="tpu_custom_call" | custom-call | tf_op jit(solution)/shard_map/pallas_call | solution.py:282
  162.8 1.3 copy.6
Async XLA Ops:
  0.0 0.7 copy-start

commit v2 on v1

--- a/solution.py
+++ b/solution.py
@@ -8,7 +8,8 @@
 from jax.sharding import PartitionSpec as P
 
 WIDTH = 128
-LAG = 4
+GROUP = 2
+LAGS = (1, 4, 4)
 
 
 def flip(index, mask):
@@ -102,11 +103,12 @@
         device_id_type=pl.DeviceIdType.MESH,
     )
 
-    load(0).start()
+    for chunk in range(GROUP):
+        load(chunk).start()
     for level in range(local_bits + 1):
         for copy in weight_loads(level):
             copy.start()
-    for chunk in range(1, chunks):
+    for chunk in range(GROUP, chunks):
         load(chunk).start()
     for level in range(local_bits + 1, levels):
         for copy in weight_loads(level):
@@ -129,70 +131,87 @@
     def masked(values, rank_tile):
         return jnp.where(row < rank_tile[0:1, :], values, 0.0)
 
-    def first(chunk):
-        base = chunk * nodes
-        load(chunk).wait()
-
-        def at(bank, node):
-            return acc.at[base + node] if bank == 0 else tmp.at[node]
-
+    def state(bank, chunk, node):
+        return acc.at[chunk * nodes + node] if bank == 0 else tmp.at[chunk % GROUP, node]
+
+    def stack(bank, pair, node):
+        halves = [split(state(bank, pair * GROUP + part, node)[...]) for part in range(GROUP)]
+        return tuple(jnp.concatenate(half, axis=1) for half in zip(*halves))
+
+    def columns(values, part):
+        return values[:, part * width : (part + 1) * width]
+
+    def local(pair):
+        for part in range(GROUP):
+            load(pair * GROUP + part).wait()
         for level in range(local_bits):
 
-            @pl.when(chunk == 0)
+            @pl.when(pair == 0)
             def _():
                 for copy in weight_loads(level):
                     copy.wait()
 
-            def body(node, _):
-                other = flip(node, 1 << level)
-                value = product(self_w[level, node], split(at(level % 2, node)[...]))
-                value += product(cross_w[level, other], split(at(level % 2, other)[...]))
-                at((level + 1) % 2, node)[...] = masked(value, own_rank[node])
-                return 0
-
-            lax.fori_loop(0, nodes, body, 0)
-
-        @pl.when(chunk == 0)
+            for node in range(nodes):
+                other = node + (1 << level)
+                if (node >> level) % 2:
+                    continue
+                mine, theirs = stack(level % 2, pair, node), stack(level % 2, pair, other)
+                for to, at, source in ((node, mine, theirs), (other, theirs, mine)):
+                    value = product(self_w[level, to], at)
+                    value += product(cross_w[level, node + other - to], source)
+                    for part in range(GROUP):
+                        state((level + 1) % 2, pair * GROUP + part, to)[...] = masked(
+                            columns(value, part), own_rank[to]
+                        )
+
+        @pl.when(pair == 0)
         def _():
             for copy in weight_loads(local_bits):
                 copy.wait()
 
-        def body(node, _):
-            parts = split(at(local_bits % 2, node)[...])
-            send[0, base + node] = product(cross_w[local_bits, node], parts)
-            hop_copy(0, base + node).start()
-            acc[base + node] = product(self_w[local_bits, node], parts)
-            return 0
-
-        lax.fori_loop(0, nodes, body, 0)
-
-    def combine(hop, item):
+    def first(step):
+        pair, node = step // nodes, step % nodes
+        parts = stack(local_bits % 2, pair, node)
+        value = product(cross_w[local_bits, node], parts)
+        for part in range(GROUP):
+            send[0, (pair * GROUP + part) * nodes + node] = columns(value, part)
+            hop_copy(0, (pair * GROUP + part) * nodes + node).start()
+        value = product(self_w[local_bits, node], parts)
+        for part in range(GROUP):
+            acc[(pair * GROUP + part) * nodes + node] = columns(value, part)
+
+    def combine(hop, item, lead):
         level = local_bits + hop
 
-        @pl.when(item == 0)
+        @pl.when(lead)
         def _():
             for copy in weight_loads(level):
                 copy.wait()
 
         hop_copy(hop - 1, item).wait_recv()
         node = item % nodes
-        return node, level, split(masked(acc[item] + recv[hop - 1, item], own_rank[node]))
-
-    def middle(hop, item):
-        node, level, parts = combine(hop, item)
-        send[hop, item] = product(cross_w[level, node], parts)
+        high, low = split(masked(acc[item] + recv[hop - 1, item], own_rank[node]))
+        return node, level, jnp.concatenate([high, low], axis=1)
+
+    def wide(weights, parts):
+        both = jnp.dot(weights, parts, preferred_element_type=jnp.float32)
+        return both[:, :width] + both[:, width:]
+
+    def middle(hop, item, lead):
+        node, level, parts = combine(hop, item, lead)
+        send[hop, item] = wide(cross_w[level, node], parts)
         hop_copy(hop, item).start()
-        acc[item] = product(self_w[level, node], parts)
-
-    def last(item):
-        node, level, parts = combine(hops - 1, item)
-
-        @pl.when(item == 0)
+        acc[item] = wide(self_w[level, node], parts)
+
+    def last(item, lead):
+        node, level, parts = combine(hops - 1, item, lead)
+
+        @pl.when(lead)
         def _():
             rank_copy.wait()
 
-        sent = masked(product(cross_w[level, node], parts), other_rank[node])
-        kept = masked(product(self_w[level, node], parts), own_rank[node])
+        sent = masked(wide(cross_w[level, node], parts), other_rank[node])
+        kept = masked(wide(self_w[level, node], parts), own_rank[node])
 
         chunk = item // nodes
         piece = chunk // cols
@@ -225,30 +244,47 @@
         start = pl.multiple_of(piece * width, width)
         out[node, :, pl.ds(start, width)] = acc[item] + end_recv[place]
 
+    steps = items // GROUP
+    slots = GROUP * (steps + GROUP - 1)
+
+    def place_of(slot):
+        part = slot % GROUP
+        step = slot // GROUP - part
+        item = (step // nodes * GROUP + part) * nodes + step % nodes
+        return (slot >= 0) & (step >= 0) & (step < steps), item
+
     def tick(time, _):
-        @pl.when((time < items) & (time % nodes == 0))
-        def _():
-            first(time // nodes)
+        step = time // GROUP
+
+        @pl.when((time % GROUP == 0) & (step < steps) & (step % nodes == 0))
+        def _():
+            local(step // nodes)
+
+        @pl.when((time % GROUP == 0) & (step < steps))
+        def _():
+            first(step)
 
         for hop in range(1, hops):
-            item = time - (1 + (hop - 1) * LAG)
-
-            @pl.when((item >= 0) & (item < items))
+            slot = time - LAGS[0] - (hop - 1) * LAGS[1]
+            held, item = place_of(slot)
+
+            @pl.when(held)
             def _():
                 if hop == hops - 1:
-                    last(item)
+                    last(item, slot == 0)
                 else:
-                    middle(hop, item)
-
-        done = time - (1 + (hops - 1) * LAG)
-
-        @pl.when((done >= 0) & ((done // nodes) % cols == cols - 1))
-        def _():
-            finish(done)
+                    middle(hop, item, slot == 0)
+
+        slot = time - LAGS[0] - (hops - 2) * LAGS[1] - LAGS[2]
+        held, item = place_of(slot)
+
+        @pl.when(held & ((item // nodes) % cols == cols - 1))
+        def _():
+            finish(item)
 
         return 0
 
-    lax.fori_loop(0, items + 1 + (hops - 1) * LAG, tick, 0)
+    lax.fori_loop(0, slots + LAGS[0] + (hops - 2) * LAGS[1] + LAGS[2], tick, 0)
 
     def drain_hops(item, _):
         for hop in range(hops - 1):
@@ -286,7 +322,7 @@
         out_specs=pl.BlockSpec(memory_space=pltpu.VMEM),
         scratch_shapes=[
             pltpu.VMEM((items, *tile), jnp.float32),
-            pltpu.VMEM((nodes, *tile), jnp.float32),
+            pltpu.VMEM((GROUP, nodes, *tile), jnp.float32),
             pltpu.VMEM((levels, nodes, rank, rank), jnp.bfloat16),
             pltpu.VMEM((levels, nodes, rank, rank), jnp.bfloat16),
             pltpu.VMEM((hops - 1, items, *tile), jnp.float32),

time: 164 us -> 159 us (0.970); the launches traced: 164 us -> 157 us
  Pallas kernels: 162 us -> 155 us
    pallas_call x1, Pallas kernels: 162 us -> 155 us  [shards(): pl.pallas_call(functools.partial(kernel, cols, nodes, levels, width, shar...]
where the time goes in v2:
time: 159 us; the launch traced here: 157 us
  Pallas kernels  155 us (97%)
  local copies, waits for them, and re-layouts  1.98 us (1%)
    pallas_call x1, Pallas kernels, shards(): pl.pallas_call(functools.partial(kernel, cols, nodes, levels, width, shar...  155 us

profile of v2, /device:TPU:0, one launch (start us, length us, event | category | flops | bytes accessed | tf_op | source)
XLA Modules:
  0.0 157.3 jit_solution(11581868737706258991)
XLA Ops:
  0.0 0.0 copy-start
  0.0 0.7 copy-done
  0.7 155.4 %shard_map.46 = f32[4,256,512]{2,1,0:T(8,128)S(1)} custom-call(f32[1,4,256,1024]{3,2,1,0:T(8,128)} %coeff.1, bf16[1,6,4,256,256]{4,3,2,1,0:T(8,128)(2,1)} %self_hbm.1, bf16[1,6,4,256,256]{4,3,2,1,0:T(8,128)(2,1)} %cross_hbm.1, s32[1,4]{1,0:T(1,128)S(1)} %copy-done), custom_call_target="tpu_custom_call" | custom-call | tf_op jit(solution)/shard_map/pallas_call | solution.py:318
  156.0 1.3 copy.6
Async XLA Ops:
  0.0 0.7 copy-start

commit v3 on v2

--- a/solution.py
+++ b/solution.py
@@ -9,7 +9,7 @@
 
 WIDTH = 128
 GROUP = 2
-LAGS = (1, 4, 4)
+LAGS = (1, 3, 4, 16)
 
 
 def flip(index, mask):
@@ -31,11 +31,11 @@
 
 def kernel(
     cols, nodes, levels, width, shard,
-    coeff, self_hbm, cross_hbm, ranks, out,
+    coeff, self_hbm, cross_hbm, ranks_hbm, out,
     acc, tmp, self_w, cross_w, send, recv, col_send, col_recv, end_send, end_recv,
-    own_rank, other_rank,
+    ranks, own_rank, other_rank,
     load_sem, weight_sem, send_sem, recv_sem, col_send_sem, col_recv_sem,
-    end_send_sem, end_recv_sem, rank_sem,
+    end_send_sem, end_recv_sem, rank_sem, rank_load_sem,
 ):
     rank_rows = acc.shape[1]
     local_bits = nodes.bit_length() - 1
@@ -103,16 +103,12 @@
         device_id_type=pl.DeviceIdType.MESH,
     )
 
+    rank_load = pltpu.make_async_copy(ranks_hbm, ranks, rank_load_sem)
+    rank_load.start()
     for chunk in range(GROUP):
         load(chunk).start()
-    for level in range(local_bits + 1):
-        for copy in weight_loads(level):
-            copy.start()
-    for chunk in range(GROUP, chunks):
-        load(chunk).start()
-    for level in range(local_bits + 1, levels):
-        for copy in weight_loads(level):
-            copy.start()
+    for copy in weight_loads(0):
+        copy.start()
 
     barrier = pltpu.get_barrier_semaphore()
     for peer in peers:
@@ -121,10 +117,12 @@
         pl.semaphore_signal(
             barrier, inc=1, device_id={"col": (my_col + step) % cols}, device_id_type=pl.DeviceIdType.MESH
         )
+    rank_load.wait()
+    for level in range(1, local_bits + 1):
+        for copy in weight_loads(level):
+            copy.start()
     for node in range(nodes):
         own_rank[node] = jnp.full(own_rank.shape[1:], ranks[0, node], jnp.int32)
-    pl.semaphore_wait(barrier, hops + cols - 1)
-    rank_copy.start()
 
     row = lax.broadcasted_iota(jnp.int32, (rank_rows, width), 0)
 
@@ -134,51 +132,52 @@
     def state(bank, chunk, node):
         return acc.at[chunk * nodes + node] if bank == 0 else tmp.at[chunk % GROUP, node]
 
-    def stack(bank, pair, node):
-        halves = [split(state(bank, pair * GROUP + part, node)[...]) for part in range(GROUP)]
+    def stack(bank, pair, node, parts):
+        halves = [split(state(bank, pair * GROUP + part, node)[...]) for part in parts]
         return tuple(jnp.concatenate(half, axis=1) for half in zip(*halves))
 
-    def columns(values, part):
-        return values[:, part * width : (part + 1) * width]
-
-    def local(pair):
-        for part in range(GROUP):
+    def wide(weights, both):
+        value = jnp.dot(weights, both, preferred_element_type=jnp.float32)
+        return value[:, :width] + value[:, width:]
+
+    def times(weights, stacked):
+        if stacked[0].shape[1] == width:
+            return wide(weights, jnp.concatenate(stacked, axis=1))
+        return product(weights, stacked)
+
+    def columns(values, at):
+        return values[:, at * width : (at + 1) * width]
+
+    def local(pair, parts, fresh):
+        for part in parts:
             load(pair * GROUP + part).wait()
         for level in range(local_bits):
-
-            @pl.when(pair == 0)
-            def _():
+            if fresh:
                 for copy in weight_loads(level):
                     copy.wait()
-
             for node in range(nodes):
                 other = node + (1 << level)
                 if (node >> level) % 2:
                     continue
-                mine, theirs = stack(level % 2, pair, node), stack(level % 2, pair, other)
+                mine, theirs = stack(level % 2, pair, node, parts), stack(level % 2, pair, other, parts)
                 for to, at, source in ((node, mine, theirs), (other, theirs, mine)):
-                    value = product(self_w[level, to], at)
-                    value += product(cross_w[level, node + other - to], source)
-                    for part in range(GROUP):
+                    value = times(self_w[level, to], at)
+                    value += times(cross_w[level, node + other - to], source)
+                    for index, part in enumerate(parts):
                         state((level + 1) % 2, pair * GROUP + part, to)[...] = masked(
-                            columns(value, part), own_rank[to]
+                            columns(value, index), own_rank[to]
                         )
 
-        @pl.when(pair == 0)
-        def _():
-            for copy in weight_loads(local_bits):
-                copy.wait()
-
-    def first(step):
+    def first(step, parts):
         pair, node = step // nodes, step % nodes
-        parts = stack(local_bits % 2, pair, node)
-        value = product(cross_w[local_bits, node], parts)
-        for part in range(GROUP):
-            send[0, (pair * GROUP + part) * nodes + node] = columns(value, part)
+        stacked = stack(local_bits % 2, pair, node, parts)
+        value = times(cross_w[local_bits, node], stacked)
+        for index, part in enumerate(parts):
+            send[0, (pair * GROUP + part) * nodes + node] = columns(value, index)
             hop_copy(0, (pair * GROUP + part) * nodes + node).start()
-        value = product(self_w[local_bits, node], parts)
-        for part in range(GROUP):
-            acc[(pair * GROUP + part) * nodes + node] = columns(value, part)
+        value = times(self_w[local_bits, node], stacked)
+        for index, part in enumerate(parts):
+            acc[(pair * GROUP + part) * nodes + node] = columns(value, index)
 
     def combine(hop, item, lead):
         level = local_bits + hop
@@ -192,10 +191,6 @@
         node = item % nodes
         high, low = split(masked(acc[item] + recv[hop - 1, item], own_rank[node]))
         return node, level, jnp.concatenate([high, low], axis=1)
-
-    def wide(weights, parts):
-        both = jnp.dot(weights, parts, preferred_element_type=jnp.float32)
-        return both[:, :width] + both[:, width:]
 
     def middle(hop, item, lead):
         node, level, parts = combine(hop, item, lead)
@@ -240,12 +235,15 @@
         node = item % nodes
         piece = item // (nodes * cols)
         place = piece * nodes + node
-        end_copy(place).wait_recv()
+        end_copy(place).wait()
         start = pl.multiple_of(piece * width, width)
         out[node, :, pl.ds(start, width)] = acc[item] + end_recv[place]
 
     steps = items // GROUP
     slots = GROUP * (steps + GROUP - 1)
+
+    def lag(hop):
+        return LAGS[0] + (min(hop, hops - 2) - 1) * LAGS[1] + sum(LAGS[2 : 4 + hop - hops])
 
     def place_of(slot):
         part = slot % GROUP
@@ -253,19 +251,34 @@
         item = (step // nodes * GROUP + part) * nodes + step % nodes
         return (slot >= 0) & (step >= 0) & (step < steps), item
 
+    local(0, (0,), True)
+    for level in range(local_bits + 1, levels):
+        for copy in weight_loads(level):
+            copy.start()
+    for copy in weight_loads(local_bits):
+        copy.wait()
+    pl.semaphore_wait(barrier, hops + cols - 1)
+    rank_copy.start()
+    first(0, (0,))
+    for chunk in range(GROUP, chunks):
+        load(chunk).start()
+    for part in range(1, GROUP):
+        local(0, (part,), False)
+        first(0, (part,))
+
     def tick(time, _):
         step = time // GROUP
 
-        @pl.when((time % GROUP == 0) & (step < steps) & (step % nodes == 0))
-        def _():
-            local(step // nodes)
-
-        @pl.when((time % GROUP == 0) & (step < steps))
-        def _():
-            first(step)
+        @pl.when((time % GROUP == 0) & (step > 0) & (step < steps) & (step % nodes == 0))
+        def _():
+            local(step // nodes, tuple(range(GROUP)), False)
+
+        @pl.when((time % GROUP == 0) & (step > 0) & (step < steps))
+        def _():
+            first(step, tuple(range(GROUP)))
 
         for hop in range(1, hops):
-            slot = time - LAGS[0] - (hop - 1) * LAGS[1]
+            slot = time - lag(hop)
             held, item = place_of(slot)
 
             @pl.when(held)
@@ -275,33 +288,27 @@
                 else:
                     middle(hop, item, slot == 0)
 
-        slot = time - LAGS[0] - (hops - 2) * LAGS[1] - LAGS[2]
+        slot = time - lag(hops)
         held, item = place_of(slot)
 
-        @pl.when(held & ((item // nodes) % cols == cols - 1))
+        chunk = item // nodes
+
+        @pl.when(held)
+        def _():
+            for hop in range(hops - 1):
+                hop_copy(hop, item).wait_send()
+
+        @pl.when(held & (chunk % cols < cols - 1))
+        def _():
+            col_copy((chunk // cols * (cols - 1) + chunk % cols) * nodes + item % nodes).wait_send()
+
+        @pl.when(held & (chunk % cols == cols - 1))
         def _():
             finish(item)
 
         return 0
 
-    lax.fori_loop(0, slots + LAGS[0] + (hops - 2) * LAGS[1] + LAGS[2], tick, 0)
-
-    def drain_hops(item, _):
-        for hop in range(hops - 1):
-            hop_copy(hop, item).wait_send()
-        return 0
-
-    def drain_cols(item, _):
-        col_copy(item).wait_send()
-        return 0
-
-    def drain_end(place, _):
-        end_copy(place).wait_send()
-        return 0
-
-    lax.fori_loop(0, items, drain_hops, 0)
-    lax.fori_loop(0, theirs, drain_cols, 0)
-    lax.fori_loop(0, items - theirs, drain_end, 0)
+    lax.fori_loop(0, slots + lag(hops), tick, 0)
 
 
 def shards(cols, coefficients, self_weights, cross_weights, true_ranks):
@@ -318,7 +325,7 @@
     return pl.pallas_call(
         functools.partial(kernel, cols, nodes, levels, width, shard),
         out_shape=jax.ShapeDtypeStruct((nodes, rank, shard), jnp.float32),
-        in_specs=[pl.BlockSpec(memory_space=pl.ANY)] * 3 + [pl.BlockSpec(memory_space=pltpu.SMEM)],
+        in_specs=[pl.BlockSpec(memory_space=pl.ANY)] * 3 + [pl.BlockSpec(memory_space=pltpu.HBM)],
         out_specs=pl.BlockSpec(memory_space=pltpu.VMEM),
         scratch_shapes=[
             pltpu.VMEM((items, *tile), jnp.float32),
@@ -331,6 +338,7 @@
             pltpu.VMEM((theirs, 2, *tile), jnp.float32),
             pltpu.VMEM((mine, *tile), jnp.float32),
             pltpu.VMEM((mine, *tile), jnp.float32),
+            pltpu.SMEM(true_ranks.shape, jnp.int32),
             pltpu.VMEM((nodes, 8, width), jnp.int32),
             pltpu.VMEM((nodes, 8, width), jnp.int32),
             dma((items // nodes,)),
@@ -342,11 +350,12 @@
             dma((mine,)),
             dma((mine,)),
             dma((2,)),
+            dma,
         ],
         compiler_params=pltpu.CompilerParams(
             collective_id=0, has_side_effects=True, vmem_limit_bytes=51 * 1024 * 1024
         ),
-    )(coefficients, self_weights, cross_weights, true_ranks)
+    )(coefficients, self_weights, cross_weights, pltpu.with_memory_space_constraint(true_ranks, pltpu.HBM))
 
 
 def solution(mesh):

time: 159 us -> 156 us (0.981)
  Pallas kernels: 155 us -> 153 us
    pallas_call x1, Pallas kernels: 155 us -> 153 us  [shards(): pl.pallas_call(functools.partial(kernel, cols, nodes, levels, width, shar...]
where the time goes in v3:
time: 156 us; the launch traced here: 154 us
  Pallas kernels  153 us (98%)
    pallas_call x1, Pallas kernels, shards(): pl.pallas_call(functools.partial(kernel, cols, nodes, levels, width, shar...  153 us

profile of v3, /device:TPU:0, one launch (start us, length us, event | category | flops | bytes accessed | tf_op | source)
XLA Modules:
  0.0 154.2 jit_solution(17978503888632431599)
XLA Ops:
  0.0 152.9 %shard_map.46 = f32[4,256,512]{2,1,0:T(8,128)S(1)} custom-call(f32[1,4,256,1024]{3,2,1,0:T(8,128)} %coeff.1, bf16[1,6,4,256,256]{4,3,2,1,0:T(8,128)(2,1)} %self_hbm.1, bf16[1,6,4,256,256]{4,3,2,1,0:T(8,128)(2,1)} %cross_hbm.1, s32[1,4]{1,0:T(1,128)} %ranks_hbm.1), custom_call_target="tpu_custom_call" | custom-call | tf_op jit(solution)/shard_map/pallas_call | solution.py:325
  152.9 1.3 copy.6

commit v4 on v3

--- a/solution.py
+++ b/solution.py
@@ -9,6 +9,7 @@
 
 WIDTH = 128
 GROUP = 2
+RING = 16
 LAGS = (1, 3, 4, 16)
 
 
@@ -63,13 +64,28 @@
             pltpu.make_async_copy(cross_hbm.at[0, level], cross_w.at[level], weight_sem.at[1, level]),
         )
 
+    def ring(item):
+        chunk = item // nodes
+        part = chunk % GROUP
+        return (GROUP * (chunk // GROUP * nodes + item % nodes + part) + part) % RING
+
     def hop_copy(hop, item):
         return pltpu.make_async_remote_copy(
             src_ref=send.at[hop, item],
             dst_ref=recv.at[hop, item],
-            send_sem=send_sem.at[hop, item],
-            recv_sem=recv_sem.at[hop, item],
+            send_sem=send_sem.at[hop],
+            recv_sem=recv_sem.at[hop, ring(item)],
             device_id={"node": peers[hop]},
+            device_id_type=pl.DeviceIdType.MESH,
+        )
+
+    def whole_copy(source, target, source_sem, target_sem):
+        return pltpu.make_async_remote_copy(
+            src_ref=source,
+            dst_ref=target,
+            send_sem=source_sem,
+            recv_sem=target_sem,
+            device_id={"node": peers[0]},
             device_id_type=pl.DeviceIdType.MESH,
         )
 
@@ -78,7 +94,7 @@
         return pltpu.make_async_remote_copy(
             src_ref=col_send.at[item],
             dst_ref=col_recv.at[item],
-            send_sem=col_send_sem.at[item],
+            send_sem=col_send_sem,
             recv_sem=col_recv_sem.at[item],
             device_id={"col": column},
             device_id_type=pl.DeviceIdType.MESH,
@@ -88,7 +104,7 @@
         return pltpu.make_async_remote_copy(
             src_ref=end_send.at[place],
             dst_ref=end_recv.at[place],
-            send_sem=end_send_sem.at[place],
+            send_sem=end_send_sem,
             recv_sem=end_recv_sem.at[place],
             device_id={"node": peers[hops - 1]},
             device_id_type=pl.DeviceIdType.MESH,
@@ -235,7 +251,7 @@
         node = item % nodes
         piece = item // (nodes * cols)
         place = piece * nodes + node
-        end_copy(place).wait()
+        end_copy(place).wait_recv()
         start = pl.multiple_of(piece * width, width)
         out[node, :, pl.ds(start, width)] = acc[item] + end_recv[place]
 
@@ -291,24 +307,18 @@
         slot = time - lag(hops)
         held, item = place_of(slot)
 
-        chunk = item // nodes
-
-        @pl.when(held)
-        def _():
-            for hop in range(hops - 1):
-                hop_copy(hop, item).wait_send()
-
-        @pl.when(held & (chunk % cols < cols - 1))
-        def _():
-            col_copy((chunk // cols * (cols - 1) + chunk % cols) * nodes + item % nodes).wait_send()
-
-        @pl.when(held & (chunk % cols == cols - 1))
+        @pl.when(held & ((item // nodes) % cols == cols - 1))
         def _():
             finish(item)
 
         return 0
 
     lax.fori_loop(0, slots + lag(hops), tick, 0)
+
+    for hop in range(hops - 1):
+        whole_copy(send.at[hop], recv.at[hop], send_sem.at[hop], recv_sem.at[hop, 0]).wait_send()
+    whole_copy(col_send, col_recv, col_send_sem, col_recv_sem.at[0]).wait_send()
+    whole_copy(end_send, end_recv, end_send_sem, end_recv_sem.at[0]).wait_send()
 
 
 def shards(cols, coefficients, self_weights, cross_weights, true_ranks):
@@ -343,11 +353,11 @@
             pltpu.VMEM((nodes, 8, width), jnp.int32),
             dma((items // nodes,)),
             dma((2, levels)),
-            dma((hops - 1, items)),
-            dma((hops - 1, items)),
+            dma((hops - 1,)),
+            dma((hops - 1, RING)),
+            dma,
             dma((theirs,)),
-            dma((theirs,)),
-            dma((mine,)),
+            dma,
             dma((mine,)),
             dma((2,)),
             dma,

time: 156 us -> 154 us (0.987)
  Pallas kernels: 153 us -> 151 us
where the time goes in v4:
time: 154 us; the launch traced here: 153 us
  Pallas kernels  151 us (98%)
    pallas_call x1, Pallas kernels, shards(): pl.pallas_call(functools.partial(kernel, cols, nodes, levels, width, shar...  151 us

profile of v4, /device:TPU:0, one launch (start us, length us, event | category | flops | bytes accessed | tf_op | source)
XLA Modules:
  0.0 152.7 jit_solution(5105083924393221792)
XLA Ops:
  0.0 151.4 %shard_map.46 = f32[4,256,512]{2,1,0:T(8,128)S(1)} custom-call(f32[1,4,256,1024]{3,2,1,0:T(8,128)} %coeff.1, bf16[1,6,4,256,256]{4,3,2,1,0:T(8,128)(2,1)} %self_hbm.1, bf16[1,6,4,256,256]{4,3,2,1,0:T(8,128)(2,1)} %cross_hbm.1, s32[1,4]{1,0:T(1,128)} %ranks_hbm.1), custom_call_target="tpu_custom_call" | custom-call | tf_op jit(solution)/shard_map/pallas_call | solution.py:335
  151.4 1.3 copy.6

commit v5 on v4

--- a/solution.py
+++ b/solution.py
@@ -9,7 +9,8 @@
 
 WIDTH = 128
 GROUP = 2
-RING = 16
+RING = 12
+COL_RING = 8
 LAGS = (1, 3, 4, 16)
 
 
@@ -55,13 +56,16 @@
         return pltpu.make_async_copy(
             coeff.at[0, :, :, pl.ds(start, width)],
             acc.at[pl.ds(chunk * nodes, nodes)],
-            load_sem.at[chunk],
-        )
-
-    def weight_loads(level):
+            load_sem.at[min(chunk, GROUP)],
+        )
+
+    bands = [(level, level + 1) for level in range(local_bits + 2)] + [(local_bits + 2, levels)]
+
+    def weight_loads(group):
+        band = pl.ds(bands[group][0], bands[group][1] - bands[group][0])
         return (
-            pltpu.make_async_copy(self_hbm.at[0, level], self_w.at[level], weight_sem.at[0, level]),
-            pltpu.make_async_copy(cross_hbm.at[0, level], cross_w.at[level], weight_sem.at[1, level]),
+            pltpu.make_async_copy(self_hbm.at[0, band], self_w.at[band], weight_sem.at[0, group]),
+            pltpu.make_async_copy(cross_hbm.at[0, band], cross_w.at[band], weight_sem.at[1, group]),
         )
 
     def ring(item):
@@ -95,7 +99,7 @@
             src_ref=col_send.at[item],
             dst_ref=col_recv.at[item],
             send_sem=col_send_sem,
-            recv_sem=col_recv_sem.at[item],
+            recv_sem=col_recv_sem.at[item // nodes % (cols - 1), (item // nodes // (cols - 1) * nodes + item % nodes) % col_recv_sem.shape[1]],
             device_id={"col": column},
             device_id_type=pl.DeviceIdType.MESH,
         )
@@ -121,8 +125,7 @@
 
     rank_load = pltpu.make_async_copy(ranks_hbm, ranks, rank_load_sem)
     rank_load.start()
-    for chunk in range(GROUP):
-        load(chunk).start()
+    load(0).start()
     for copy in weight_loads(0):
         copy.start()
 
@@ -134,9 +137,11 @@
             barrier, inc=1, device_id={"col": (my_col + step) % cols}, device_id_type=pl.DeviceIdType.MESH
         )
     rank_load.wait()
-    for level in range(1, local_bits + 1):
-        for copy in weight_loads(level):
+    for group in range(1, local_bits + 1):
+        for copy in weight_loads(group):
             copy.start()
+    for part in range(1, GROUP):
+        load(part).start()
     for node in range(nodes):
         own_rank[node] = jnp.full(own_rank.shape[1:], ranks[0, node], jnp.int32)
 
@@ -164,17 +169,17 @@
     def columns(values, at):
         return values[:, at * width : (at + 1) * width]
 
-    def local(pair, parts, fresh):
-        for part in parts:
-            load(pair * GROUP + part).wait()
-        for level in range(local_bits):
-            if fresh:
-                for copy in weight_loads(level):
-                    copy.wait()
-            for node in range(nodes):
+    def lower(level):
+        return [node for node in range(nodes) if (node >> level) % 2 == 0]
+
+    every = [(level, lower(level)) for level in range(local_bits)]
+    early = every[:-1] + [(local_bits - 1, [0])]
+    late = [(local_bits - 1, lower(local_bits - 1)[1:])]
+
+    def local(pair, parts, stages):
+        for level, chosen in stages:
+            for node in chosen:
                 other = node + (1 << level)
-                if (node >> level) % 2:
-                    continue
                 mine, theirs = stack(level % 2, pair, node, parts), stack(level % 2, pair, other, parts)
                 for to, at, source in ((node, mine, theirs), (other, theirs, mine)):
                     value = times(self_w[level, to], at)
@@ -198,10 +203,12 @@
     def combine(hop, item, lead):
         level = local_bits + hop
 
-        @pl.when(lead)
-        def _():
-            for copy in weight_loads(level):
-                copy.wait()
+        if level < len(bands):
+
+            @pl.when(lead)
+            def _():
+                for copy in weight_loads(level):
+                    copy.wait()
 
         hop_copy(hop - 1, item).wait_recv()
         node = item % nodes
@@ -222,30 +229,30 @@
             rank_copy.wait()
 
         sent = masked(wide(cross_w[level, node], parts), other_rank[node])
-        kept = masked(wide(self_w[level, node], parts), own_rank[node])
-
         chunk = item // nodes
         piece = chunk // cols
 
         @pl.when(chunk % cols < cols - 1)
         def _():
             slot = (piece * (cols - 1) + chunk % cols) * nodes + node
-            col_send[slot, 0] = kept
             col_send[slot, 1] = sent
+            col_send[slot, 0] = masked(wide(self_w[level, node], parts), own_rank[node])
             col_copy(slot).start()
 
         @pl.when(chunk % cols == cols - 1)
         def _():
             place = piece * nodes + node
-            total_kept, total_sent = kept, sent
+            first_slot = piece * (cols - 1) * nodes + node
+            total = sent
             for step in range(cols - 1):
-                slot = (piece * (cols - 1) + step) * nodes + node
-                col_copy(slot).wait_recv()
-                total_kept += col_recv[slot, 0]
-                total_sent += col_recv[slot, 1]
-            end_send[place] = total_sent
+                col_copy(first_slot + step * nodes).wait_recv()
+                total += col_recv[first_slot + step * nodes, 1]
+            end_send[place] = total
             end_copy(place).start()
-            acc[item] = total_kept
+            total = masked(wide(self_w[level, node], parts), own_rank[node])
+            for step in range(cols - 1):
+                total += col_recv[first_slot + step * nodes, 0]
+            acc[item] = total
 
     def finish(item):
         node = item % nodes
@@ -267,9 +274,13 @@
         item = (step // nodes * GROUP + part) * nodes + step % nodes
         return (slot >= 0) & (step >= 0) & (step < steps), item
 
-    local(0, (0,), True)
-    for level in range(local_bits + 1, levels):
+    load(0).wait()
+    for level, chosen in early:
         for copy in weight_loads(level):
+            copy.wait()
+        local(0, (0,), [(level, chosen)])
+    for group in range(local_bits + 1, len(bands)):
+        for copy in weight_loads(group):
             copy.start()
     for copy in weight_loads(local_bits):
         copy.wait()
@@ -278,16 +289,18 @@
     first(0, (0,))
     for chunk in range(GROUP, chunks):
         load(chunk).start()
-    for part in range(1, GROUP):
-        local(0, (part,), False)
-        first(0, (part,))
-
+    local(0, (0,), late)
     def tick(time, _):
         step = time // GROUP
 
         @pl.when((time % GROUP == 0) & (step > 0) & (step < steps) & (step % nodes == 0))
         def _():
-            local(step // nodes, tuple(range(GROUP)), False)
+            @pl.when(step == nodes)
+            def _():
+                rest = pl.ds(GROUP * nodes, (chunks - GROUP) * nodes)
+                pltpu.make_async_copy(acc.at[rest], acc.at[rest], load_sem.at[GROUP]).wait()
+
+            local(step // nodes, tuple(range(GROUP)), every)
 
         @pl.when((time % GROUP == 0) & (step > 0) & (step < steps))
         def _():
@@ -304,6 +317,13 @@
                 else:
                     middle(hop, item, slot == 0)
 
+        @pl.when(time == LAGS[0])
+        def _():
+            for part in range(1, GROUP):
+                load(part).wait()
+                local(0, (part,), every)
+                first(0, (part,))
+
         slot = time - lag(hops)
         held, item = place_of(slot)
 
@@ -317,7 +337,7 @@
 
     for hop in range(hops - 1):
         whole_copy(send.at[hop], recv.at[hop], send_sem.at[hop], recv_sem.at[hop, 0]).wait_send()
-    whole_copy(col_send, col_recv, col_send_sem, col_recv_sem.at[0]).wait_send()
+    whole_copy(col_send, col_recv, col_send_sem, col_recv_sem.at[0, 0]).wait_send()
     whole_copy(end_send, end_recv, end_send_sem, end_recv_sem.at[0]).wait_send()
 
 
@@ -351,12 +371,12 @@
             pltpu.SMEM(true_ranks.shape, jnp.int32),
             pltpu.VMEM((nodes, 8, width), jnp.int32),
             pltpu.VMEM((nodes, 8, width), jnp.int32),
-            dma((items // nodes,)),
-            dma((2, levels)),
+            dma((GROUP + 1,)),
+            dma((2, nodes.bit_length() + 2)),
             dma((hops - 1,)),
             dma((hops - 1, RING)),
             dma,
-            dma((theirs,)),
+            dma((cols - 1, min(COL_RING, mine))),
             dma,
             dma((mine,)),
             dma((2,)),

time: 154 us -> 154 us (level)
  no operation moved by 1% of the time
where the time goes in v5:
time: 154 us; the launch traced here: 153 us
  Pallas kernels  151 us (98%)
    pallas_call x1, Pallas kernels, shards(): pl.pallas_call(functools.partial(kernel, cols, nodes, levels, width, shar...  151 us

profile of v5, /device:TPU:0, one launch (start us, length us, event | category | flops | bytes accessed | tf_op | source)
XLA Modules:
  0.0 152.6 jit_solution(9722394329974153981)
XLA Ops:
  0.0 151.3 %shard_map.46 = f32[4,256,512]{2,1,0:T(8,128)S(1)} custom-call(f32[1,4,256,1024]{3,2,1,0:T(8,128)} %coeff.1, bf16[1,6,4,256,256]{4,3,2,1,0:T(8,128)(2,1)} %self_hbm.1, bf16[1,6,4,256,256]{4,3,2,1,0:T(8,128)(2,1)} %cross_hbm.1, s32[1,4]{1,0:T(1,128)} %ranks_hbm.1), custom_call_target="tpu_custom_call" | custom-call | tf_op jit(solution)/shard_map/pallas_call | solution.py:355
  151.3 1.3 copy.6

commit v6 on v5

--- a/solution.py
+++ b/solution.py
@@ -35,9 +35,10 @@
     cols, nodes, levels, width, shard,
     coeff, self_hbm, cross_hbm, ranks_hbm, out,
     acc, tmp, self_w, cross_w, send, recv, col_send, col_recv, end_send, end_recv,
+    tail_send, tail_recv, tail_keep,
     ranks, own_rank, other_rank,
     load_sem, weight_sem, send_sem, recv_sem, col_send_sem, col_recv_sem,
-    end_send_sem, end_recv_sem, rank_sem, rank_load_sem,
+    end_send_sem, end_recv_sem, rank_sem, rank_load_sem, tail_sem,
 ):
     rank_rows = acc.shape[1]
     local_bits = nodes.bit_length() - 1
@@ -90,6 +91,16 @@
             send_sem=source_sem,
             recv_sem=target_sem,
             device_id={"node": peers[0]},
+            device_id_type=pl.DeviceIdType.MESH,
+        )
+
+    def half_copy(stage, half):
+        return pltpu.make_async_remote_copy(
+            src_ref=tail_send.at[stage, half],
+            dst_ref=tail_recv.at[stage, half],
+            send_sem=tail_sem.at[0, stage, half],
+            recv_sem=tail_sem.at[1, stage, half],
+            device_id={"node": peers[hops - 2 + stage]},
             device_id_type=pl.DeviceIdType.MESH,
         )
 
@@ -215,10 +226,67 @@
         high, low = split(masked(acc[item] + recv[hop - 1, item], own_rank[node]))
         return node, level, jnp.concatenate([high, low], axis=1)
 
+    def lanes(values, half):
+        return values[:, half * (width // 2) : (half + 1) * (width // 2)]
+
+    def fold(values):
+        return jnp.concatenate([values[: rank_rows // 2], values[rank_rows // 2 :]], axis=1)
+
+    def unfold(tile):
+        return jnp.concatenate([lanes(tile, 0), lanes(tile, 1)], axis=0)
+
+    def half_wide(weights, both, rank_tile):
+        value = wide_dot(weights, both)
+        value = lanes(value, 0) + lanes(value, 1)
+        return jnp.where(row[:, : width // 2] < rank_tile[0:1, : width // 2], value, 0.0)
+
+    def wide_dot(weights, both):
+        return jnp.dot(weights, both, preferred_element_type=jnp.float32)
+
+    def tail_last():
+        item, node, level = items - 1, nodes - 1, levels - 1
+        slots_in = [((pieces - 1) * (cols - 1) + step) * nodes + node for step in range(cols - 1)]
+        for half in range(2):
+            half_copy(0, half).wait_recv()
+            value = lanes(acc[item], half) + unfold(tail_recv[0, half])
+            value = jnp.where(row[:, : width // 2] < own_rank[node][0:1, : width // 2], value, 0.0)
+            both = jnp.concatenate(split(value), axis=1)
+            total = half_wide(cross_w[level, node], both, other_rank[node])
+            for slot in slots_in:
+                if half == 0:
+                    col_copy(slot).wait_recv()
+                total += lanes(col_recv[slot, 1], half)
+            tail_send[1, half] = fold(total)
+            half_copy(1, half).start()
+            total = half_wide(self_w[level, node], both, own_rank[node])
+            for slot in slots_in:
+                total += lanes(col_recv[slot, 0], half)
+            tail_keep[half] = total
+
+    def tail_finish():
+        values = []
+        for half in range(2):
+            half_copy(1, half).wait_recv()
+            values.append(tail_keep[half] + unfold(tail_recv[1, half]))
+        out[nodes - 1, :, pl.ds((pieces - 1) * width, width)] = jnp.concatenate(values, axis=1)
+
     def middle(hop, item, lead):
         node, level, parts = combine(hop, item, lead)
-        send[hop, item] = wide(cross_w[level, node], parts)
-        hop_copy(hop, item).start()
+        value = wide(cross_w[level, node], parts)
+
+        @pl.when((item < items - 1) | (hop < hops - 2))
+        def _():
+            send[hop, item] = value
+            hop_copy(hop, item).start()
+
+        if hop == hops - 2:
+
+            @pl.when(item == items - 1)
+            def _():
+                for half in range(2):
+                    tail_send[0, half] = fold(lanes(value, half))
+                    half_copy(0, half).start()
+
         acc[item] = wide(self_w[level, node], parts)
 
     def last(item, lead):
@@ -310,11 +378,20 @@
             slot = time - lag(hop)
             held, item = place_of(slot)
 
-            @pl.when(held)
-            def _():
-                if hop == hops - 1:
+            if hop == hops - 1:
+
+                @pl.when(held & (item < items - 1))
+                def _():
                     last(item, slot == 0)
-                else:
+
+                @pl.when(held & (item == items - 1))
+                def _():
+                    tail_last()
+
+            else:
+
+                @pl.when(held)
+                def _():
                     middle(hop, item, slot == 0)
 
         @pl.when(time == LAGS[0])
@@ -327,18 +404,27 @@
         slot = time - lag(hops)
         held, item = place_of(slot)
 
-        @pl.when(held & ((item // nodes) % cols == cols - 1))
+        @pl.when(held & ((item // nodes) % cols == cols - 1) & (item < items - 1))
         def _():
             finish(item)
 
+        @pl.when(held & (item == items - 1))
+        def _():
+            tail_finish()
+
         return 0
 
     lax.fori_loop(0, slots + lag(hops), tick, 0)
 
     for hop in range(hops - 1):
-        whole_copy(send.at[hop], recv.at[hop], send_sem.at[hop], recv_sem.at[hop, 0]).wait_send()
+        sent = pl.ds(0, items - hop // (hops - 2))
+        whole_copy(send.at[hop, sent], recv.at[hop, sent], send_sem.at[hop], recv_sem.at[hop, 0]).wait_send()
     whole_copy(col_send, col_recv, col_send_sem, col_recv_sem.at[0, 0]).wait_send()
-    whole_copy(end_send, end_recv, end_send_sem, end_recv_sem.at[0]).wait_send()
+    sent = pl.ds(0, items - theirs - 1)
+    whole_copy(end_send.at[sent], end_recv.at[sent], end_send_sem, end_recv_sem.at[0]).wait_send()
+    for stage in range(2):
+        for half in range(2):
+            half_copy(stage, half).wait_send()
 
 
 def shards(cols, coefficients, self_weights, cross_weights, true_ranks):
@@ -368,6 +454,9 @@
             pltpu.VMEM((theirs, 2, *tile), jnp.float32),
             pltpu.VMEM((mine, *tile), jnp.float32),
             pltpu.VMEM((mine, *tile), jnp.float32),
+            pltpu.VMEM((2, 2, rank // 2, width), jnp.float32),
+            pltpu.VMEM((2, 2, rank // 2, width), jnp.float32),
+            pltpu.VMEM((2, rank, width // 2), jnp.float32),
             pltpu.SMEM(true_ranks.shape, jnp.int32),
             pltpu.VMEM((nodes, 8, width), jnp.int32),
             pltpu.VMEM((nodes, 8, width), jnp.int32),
@@ -381,9 +470,10 @@
             dma((mine,)),
             dma((2,)),
             dma,
+            dma((2, 2, 2)),
         ],
         compiler_params=pltpu.CompilerParams(
-            collective_id=0, has_side_effects=True, vmem_limit_bytes=51 * 1024 * 1024
+            collective_id=0, has_side_effects=True, vmem_limit_bytes=53 * 1024 * 1024
         ),
     )(coefficients, self_weights, cross_weights, pltpu.with_memory_space_constraint(true_ranks, pltpu.HBM))
 

time: 154 us -> 157 us (1.019)
  Pallas kernels: 151 us -> 153 us
  local copies, waits for them, and re-layouts: 1.32 us -> 3.08 us
    pallas_call x1, Pallas kernels: 151 us -> 153 us  [shards(): pl.pallas_call(functools.partial(kernel, cols, nodes, levels, width, shar...]
    unnamed x1, local copies, waits for them, and re-layouts: 1.32 us -> 3.08 us
where the time goes in v6:
time: 157 us; the launch traced here: 156 us
  Pallas kernels  153 us (97%)
  local copies, waits for them, and re-layouts  3.08 us (2%)
    pallas_call x1, Pallas kernels, shards(): pl.pallas_call(functools.partial(kernel, cols, nodes, levels, width, shar...  153 us

profile of v6, /device:TPU:0, one launch (start us, length us, event | category | flops | bytes accessed | tf_op | source)
XLA Modules:
  0.0 156.4 jit_solution(14617135406923192319)
XLA Ops:
  0.0 153.4 %shard_map.46 = f32[4,256,512]{2,1,0:T(8,128)} custom-call(f32[1,4,256,1024]{3,2,1,0:T(8,128)} %coeff.1, bf16[1,6,4,256,256]{4,3,2,1,0:T(8,128)(2,1)} %self_hbm.1, bf16[1,6,4,256,256]{4,3,2,1,0:T(8,128)(2,1)} %cross_hbm.1, s32[1,4]{1,0:T(1,128)} %ranks_hbm.1), custom_call_target="tpu_custom_call" | custom-call | tf_op jit(solution)/shard_map/pallas_call | solution.py:441
  153.4 3.1 %copy.6 = f32[4,256,512]{2,1,0:T(8,128)} copy(f32[4,256,512]{2,1,0:T(8,128)} %shard_map.46) | data formatting | bytes 4194304

commit v7 on v6

--- a/solution.py
+++ b/solution.py
@@ -35,7 +35,7 @@
     cols, nodes, levels, width, shard,
     coeff, self_hbm, cross_hbm, ranks_hbm, out,
     acc, tmp, self_w, cross_w, send, recv, col_send, col_recv, end_send, end_recv,
-    tail_send, tail_recv, tail_keep,
+    tail_send, tail_recv,
     ranks, own_rank, other_rank,
     load_sem, weight_sem, send_sem, recv_sem, col_send_sem, col_recv_sem,
     end_send_sem, end_recv_sem, rank_sem, rank_load_sem, tail_sem,
@@ -261,13 +261,13 @@
             total = half_wide(self_w[level, node], both, own_rank[node])
             for slot in slots_in:
                 total += lanes(col_recv[slot, 0], half)
-            tail_keep[half] = total
+            tmp[half, 0, pl.ds(0, rank_rows // 2)] = fold(total)
 
     def tail_finish():
         values = []
         for half in range(2):
             half_copy(1, half).wait_recv()
-            values.append(tail_keep[half] + unfold(tail_recv[1, half]))
+            values.append(unfold(tmp[half, 0, pl.ds(0, rank_rows // 2)] + tail_recv[1, half]))
         out[nodes - 1, :, pl.ds((pieces - 1) * width, width)] = jnp.concatenate(values, axis=1)
 
     def middle(hop, item, lead):
@@ -456,7 +456,6 @@
             pltpu.VMEM((mine, *tile), jnp.float32),
             pltpu.VMEM((2, 2, rank // 2, width), jnp.float32),
             pltpu.VMEM((2, 2, rank // 2, width), jnp.float32),
-            pltpu.VMEM((2, rank, width // 2), jnp.float32),
             pltpu.SMEM(true_ranks.shape, jnp.int32),
             pltpu.VMEM((nodes, 8, width), jnp.int32),
             pltpu.VMEM((nodes, 8, width), jnp.int32),
@@ -473,7 +472,7 @@
             dma((2, 2, 2)),
         ],
         compiler_params=pltpu.CompilerParams(
-            collective_id=0, has_side_effects=True, vmem_limit_bytes=53 * 1024 * 1024
+            collective_id=0, has_side_effects=True, vmem_limit_bytes=53 * 1024 * 1024 - nodes * rank * shard * 4
         ),
     )(coefficients, self_weights, cross_weights, pltpu.with_memory_space_constraint(true_ranks, pltpu.HBM))
 

time: 157 us -> 154 us (0.981)
  local copies, waits for them, and re-layouts: 3.08 us -> 1.32 us
    unnamed x1, local copies, waits for them, and re-layouts: 3.08 us -> 1.32 us
where the time goes in v7:
time: 154 us; the launch traced here: 153 us
  Pallas kernels  152 us (99%)
    pallas_call x1, Pallas kernels, shards(): pl.pallas_call(functools.partial(kernel, cols, nodes, levels, width, shar...  152 us

profile of v7, /device:TPU:0, one launch (start us, length us, event | category | flops | bytes accessed | tf_op | source)
XLA Modules:
  0.0 153.5 jit_solution(9717303869143937948)
XLA Ops:
  0.0 152.1 %shard_map.46 = f32[4,256,512]{2,1,0:T(8,128)S(1)} custom-call(f32[1,4,256,1024]{3,2,1,0:T(8,128)} %coeff.1, bf16[1,6,4,256,256]{4,3,2,1,0:T(8,128)(2,1)} %self_hbm.1, bf16[1,6,4,256,256]{4,3,2,1,0:T(8,128)(2,1)} %cross_hbm.1, s32[1,4]{1,0:T(1,128)} %ranks_hbm.1), custom_call_target="tpu_custom_call" | custom-call | tf_op jit(solution)/shard_map/pallas_call | solution.py:441
  152.1 1.3 copy.6

commit v8 on v7

--- a/solution.py
+++ b/solution.py
@@ -9,9 +9,9 @@
 
 WIDTH = 128
 GROUP = 2
-RING = 12
+RING = 14
 COL_RING = 8
-LAGS = (1, 3, 4, 16)
+LAGS = (1, 3, 5, 14)
 
 
 def flip(index, mask):

time: 154 us -> 154 us (level)
  no operation moved by 1% of the time
where the time goes in v8:
time: 154 us; the launch traced here: 153 us
  Pallas kernels  152 us (99%)
    pallas_call x1, Pallas kernels, shards(): pl.pallas_call(functools.partial(kernel, cols, nodes, levels, width, shar...  152 us

profile of v8, /device:TPU:0, one launch (start us, length us, event | category | flops | bytes accessed | tf_op | source)
XLA Modules:
  0.0 153.2 jit_solution(6501312214258842997)
XLA Ops:
  0.0 151.9 %shard_map.46 = f32[4,256,512]{2,1,0:T(8,128)S(1)} custom-call(f32[1,4,256,1024]{3,2,1,0:T(8,128)} %coeff.1, bf16[1,6,4,256,256]{4,3,2,1,0:T(8,128)(2,1)} %self_hbm.1, bf16[1,6,4,256,256]{4,3,2,1,0:T(8,128)(2,1)} %cross_hbm.1, s32[1,4]{1,0:T(1,128)} %ranks_hbm.1), custom_call_target="tpu_custom_call" | custom-call | tf_op jit(solution)/shard_map/pallas_call | solution.py:441
  151.9 1.3 copy.6
